TPU v7x, 32 devices: a whole 2x2x4 slice. The times are simulated.
32 devices in a mesh: gx: 4 (over y, x), gy: 2 (over core), gz: 4 (over z).
Axes of the slice: x: 2, y: 2, z: 4, core: 2. Of those that a mesh axis runs over, the one named last changes fastest.
Arguments:
- populations: float32 [2, 19, 16, 32, 512], P(None, None, 'gx', 'gy', 'gz'), may hold values from 0.01 to 0.2
- solid: int32 [16, 32, 512], P('gx', 'gy', 'gz'), may hold values 0 or 1
Outputs:
- read: float32 [2, 19, 16, 32, 512], P(None, None, 'gx', 'gy', 'gz')
All inputs are finite; a program needn't handle non-finite values. No bound on the sum of `solid` on one device may be relied on, other than what follows from the above.
Results may differ from a plain program's by a relative error of at most 0.0001.
Values sent between devices are 32-bit elements; how exact they have to be, the bound alone decides.
A program may use at most 64 MiB of HBM per device.

v0:
```python
import jax
import jax.numpy as jnp
import numpy as np
from jax import lax
from jax.sharding import PartitionSpec as P

VELOCITIES = [
    (0, 0, 0),
    (1, 0, 0),
    (-1, 0, 0),
    (0, 1, 0),
    (0, -1, 0),
    (0, 0, 1),
    (0, 0, -1),
    (1, 1, 0),
    (-1, -1, 0),
    (1, -1, 0),
    (-1, 1, 0),
    (1, 0, 1),
    (-1, 0, -1),
    (1, 0, -1),
    (-1, 0, 1),
    (0, 1, 1),
    (0, -1, -1),
    (0, 1, -1),
    (0, -1, 1),
]
WEIGHTS = [1.0 / 3.0] + [1.0 / 18.0] * 6 + [1.0 / 36.0] * 12
OPPOSITE = [0, 2, 1, 4, 3, 6, 5, 8, 7, 10, 9, 12, 11, 14, 13, 16, 15, 18, 17]
coupling = 0.9
relax_times = (1.0, 0.8)
wall_values = (0.3, 1.5)


def extended(block, sides, width):
    for axis, dim in sides:
        count = lax.axis_size(axis)
        forward = [(i, i + 1) for i in range(count - 1)]
        forward.append((count - 1, 0))
        backward = [(target, source) for source, target in forward]
        low = lax.ppermute(
            lax.slice_in_dim(block, block.shape[dim] - width, None, axis=dim), axis, forward
        )
        high = lax.ppermute(lax.slice_in_dim(block, 0, width, axis=dim), axis, backward)
        block = jnp.concatenate([low, block, high], axis=dim)
    return block


def collide(populations, fluid, psi, gradient):
    vel = jnp.asarray(np.array(VELOCITIES, np.float32))
    weights = jnp.asarray(np.array(WEIGHTS, np.float32))
    rho = jnp.sum(populations, axis=1)
    moment = jnp.einsum("ia,kixyz->kaxyz", vel, populations, precision=lax.Precision.HIGHEST)
    inv_first = 1.0 / relax_times[0]
    inv_second = 1.0 / relax_times[1]
    weight_sum = rho[0] * inv_first + rho[1] * inv_second
    common = (moment[0] * inv_first + moment[1] * inv_second) / weight_sum[None]
    forces = (-coupling * psi[0][None] * gradient[1], -coupling * psi[1][None] * gradient[0])
    results = []
    for comp in range(2):
        velocity = common + relax_times[comp] * forces[comp] / rho[comp][None]
        along = jnp.einsum("ia,axyz->ixyz", vel, velocity, precision=lax.Precision.HIGHEST)
        speed_sq = jnp.sum(velocity * velocity, axis=0)
        equil = (
            weights[:, None, None, None]
            * rho[comp][None]
            * (1.0 + 3.0 * along + 4.5 * along * along - 1.5 * speed_sq[None])
        )
        current = populations[comp]
        results.append(current - (current - equil) / relax_times[comp])
    post = jnp.stack(results, axis=0)
    return jnp.where(fluid[None, None], post, populations)


def window(padded, offset, dim_first, sizes):
    out = padded
    for axis_idx in range(3):
        start = 1 + offset[axis_idx]
        out = lax.slice_in_dim(out, start, start + sizes[axis_idx], axis=dim_first + axis_idx)
    return out


def body(populations, solid):
    fluid = solid == 0
    sizes = solid.shape
    rho = jnp.sum(populations, axis=1)
    wall = jnp.asarray(np.array(wall_values, np.float32)).reshape(2, 1, 1, 1)
    psi = jnp.where(fluid[None], rho, wall)
    signed = jnp.where(fluid[None], psi, -psi)
    padded = extended(signed, (("gx", 1), ("gy", 2), ("gz", 3)), 1)
    psi_padded = jnp.abs(padded)
    fluid_padded = padded[0] > 0.0
    parts = [jnp.zeros_like(psi) for axis_idx in range(3)]
    for i in range(1, 19):
        move = VELOCITIES[i]
        beside = window(psi_padded, move, 1, sizes)
        for axis_idx in range(3):
            if move[axis_idx] != 0:
                parts[axis_idx] = parts[axis_idx] + WEIGHTS[i] * move[axis_idx] * beside
    gradient = jnp.stack(parts, axis=1)
    post = collide(populations, fluid, psi, gradient)
    halo_post = extended(post, (("gx", 2), ("gy", 3), ("gz", 4)), 1)
    pulled_all = jnp.stack(
        [
            window(
                halo_post[:, i], (-VELOCITIES[i][0], -VELOCITIES[i][1], -VELOCITIES[i][2]), 1, sizes
            )
            for i in range(19)
        ],
        axis=1,
    )
    moved = []
    for i in range(19):
        move = VELOCITIES[i]
        source_fluid = window(fluid_padded, (-move[0], -move[1], -move[2]), 0, sizes)
        moved.append(jnp.where(source_fluid[None], pulled_all[:, i], post[:, OPPOSITE[i]]))
    result = jnp.stack(moved, axis=1)
    return jnp.where(fluid[None, None], result, populations)


def solution(mesh):
    in_specs = (P(None, None, "gx", "gy", "gz"), P("gx", "gy", "gz"))
    out_specs = P(None, None, "gx", "gy", "gz")
    return jax.shard_map(body, mesh=mesh, in_specs=in_specs, out_specs=out_specs, check_vma=False)
```

profile of v0, /device:TPU:0, one launch (start us, length us, event | category | flops | bytes accessed | tf_op | source)
XLA Modules:
  0.0 80.5 jit_solution(17574721506651843226)
XLA Ops:
  0.0 0.9 %broadcast_compare_fusion = pred[4,16,128]{2,1,0:T(8,128)(4,1)S(1)} fusion(s32[4,16,128]{2,1,0:T(8,128)} %param.6), kind=kLoop, calls=%fused_computation.187 | loop fusion | flops 8192 | bytes 40960 | tf_op jit(solution)/shard_map/eq | solution.py:84
  0.9 1.4 %reduce_sum.27 = f32[2,4,16,128]{3,2,1,0:T(8,128)S(1)} reduce(f32[2,19,4,16,128]{4,3,2,1,0:T(8,128)} %param.5, f32[]{:T(128)} %constant.17.clone.1), dimensions={1}, to_apply=%region_0.0 | reduce | flops 294912 | bytes 1310724 | tf_op jit(solution)/shard_map/reduce_sum | solution.py:86
  2.4 3.0 %collective-permute-start = (f32[2,1,16,128]{3,2,1,0:T(8,128)S(1)}, f32[2,1,16,128]{3,2,1,0:T(8,128)S(1)}, u32[]{:S(2)}, u32[]{:S(2)}) collective-permute-start(f32[2,1,16,128]{3,2,1,0:T(8,128)S(1)} %get-tuple-element.49), channel_id=1, source_target_pairs={{0,8},{8,16},{16,24},{24,0},{1,9},{9,17},{17,25},{25,1},{2,10},{10... | collective-permute-start | bytes 49160 | tf_op jit(solution)/shard_map/ppermute | solution.py:41
  5.4 1.0 %collective-permute-start.1 = (f32[2,1,16,128]{3,2,1,0:T(8,128)S(1)}, f32[2,1,16,128]{3,2,1,0:T(8,128)S(1)}, u32[]{:S(2)}, u32[]{:S(2)}) collective-permute-start(f32[2,1,16,128]{3,2,1,0:T(8,128)S(1)} %get-tuple-element.50), channel_id=1, source_target_pairs={{8,0},{16,8},{24,16},{0,24},{9,1},{17,9},{25,17},{1,25},{10,2},{18... | collective-permute-start | bytes 49160 | tf_op jit(solution)/shard_map/ppermute | solution.py:44
  6.4 1.6 %convolution_bitcast_fusion = f32[2,3,4,16,128]{4,1,3,2,0:T(4,128)S(1)} fusion(f32[19,3,1,1,1]{0,1,4,3,2:T(4,128)S(1)} %copy-done.22, f32[2,19,4,16,128]{4,3,2,1,0:T(8,128)S(1)} %copy-done), kind=kOutput, calls=%fused_computation.7 | convolution fusion | flops 11206656 | bytes 1442020 | tf_op jit(solution)/shard_map/ia,kixyz->kaxyz/dot_general | solution.py:53
  8.0 1.1 %collective-permute-done.1 = f32[2,1,16,128]{3,2,1,0:T(8,128)S(1)} collective-permute-done((f32[2,1,16,128]{3,2,1,0:T(8,128)S(1)}, f32[2,1,16,128]{3,2,1,0:T(8,128)S(1)}, u32[]{:S(2)}, u32[]{:S(2)}) %collective-permute-start.1) | collective-permute-done | bytes 16416 | tf_op jit(solution)/shard_map/ppermute | solution.py:44
  9.7 0.7 collective-permute-done.2
  10.7 1.6 %collective-permute-start.4 = (f32[2,6,18,1]{3,2,1,0:T(8,128)S(1)}, f32[2,6,18,1]{3,2,1,0:T(8,128)S(1)}, u32[]{:S(2)}, u32[]{:S(2)}) collective-permute-start(f32[2,6,18,1]{3,2,1,0:T(8,128)S(1)} %get-tuple-element.38), channel_id=1, source_target_pairs={{0,1},{1,2},{2,3},{3,0},{4,5},{5,6},{6,7},{7,4},{8,9},{9,10},{10,1... | collective-permute-start | bytes 2600 | tf_op jit(solution)/shard_map/ppermute | solution.py:41
  12.3 2.2 %collective-permute-start.5 = (f32[2,6,18,1]{3,2,1,0:T(8,128)S(1)}, f32[2,6,18,1]{3,2,1,0:T(8,128)S(1)}, u32[]{:S(2)}, u32[]{:S(2)}) collective-permute-start(f32[2,6,18,1]{3,2,1,0:T(8,128)S(1)} %get-tuple-element.39), channel_id=1, source_target_pairs={{1,0},{2,1},{3,2},{0,3},{5,4},{6,5},{7,6},{4,7},{9,8},{10,9},{11,1... | collective-permute-start | bytes 2600 | tf_op jit(solution)/shard_map/ppermute | solution.py:44
  14.5 0.7 copy.36
  15.3 4.0 %collective-permute-done.4 = f32[2,6,18,1]{3,2,1,0:T(8,128)S(1)} collective-permute-done((f32[2,6,18,1]{3,2,1,0:T(8,128)S(1)}, f32[2,6,18,1]{3,2,1,0:T(8,128)S(1)}, u32[]{:S(2)}, u32[]{:S(2)}) %collective-permute-start.4) | collective-permute-done | bytes 896 | tf_op jit(solution)/shard_map/ppermute | solution.py:41
  19.3 2.0 %collective-permute-done.5 = f32[2,6,18,1]{3,2,1,0:T(8,128)S(1)} collective-permute-done((f32[2,6,18,1]{3,2,1,0:T(8,128)S(1)}, f32[2,6,18,1]{3,2,1,0:T(8,128)S(1)}, u32[]{:S(2)}, u32[]{:S(2)}) %collective-permute-start.5) | collective-permute-done | bytes 896 | tf_op jit(solution)/shard_map/ppermute | solution.py:44
  22.6 1.1 %fusion.10 = f32[1,19,4,16,128]{4,1,3,2,0:T(8,128)S(1)} fusion(f32[2,19,4,16,128]{4,1,3,2,0:T(8,128)S(1)} %copy.36, f32[19,3,1,1]{0,1,3,2:T(4,128)S(1)} %copy-done.24, f32[3,4,16,128]{3,0,2,1:T(4,128)S(1)} %get-tuple-element.37, f32[4,16,128]{2,1,0:T(8,128)S(1)} %get-tuple-element.70, f32[4,16,128]{2,1,0:T(8,128)S(1)} %get-tuple-element.47, ...), kind=kOutput, calls=%fused_computation.18 | convolution fusion | flops 7315456 | bytes 1409328 | tf_op jit(solution)/shard_map/ia,axyz->ixyz/dot_general | solution.py:62
  23.8 1.1 %fusion.3 = f32[1,19,4,16,128]{4,1,3,2,0:T(8,128)S(1)} fusion(f32[2,19,4,16,128]{4,1,3,2,0:T(8,128)S(1)} %copy.36, f32[19,3,1,1]{0,1,3,2:T(4,128)S(1)} %copy-done.24, f32[3,4,16,128]{3,0,2,1:T(4,128)S(1)} %get-tuple-element.6, f32[4,16,128]{2,1,0:T(8,128)S(1)} %get-tuple-element.71, f32[4,16,128]{2,1,0:T(8,128)S(1)} %get-tuple-element.46, f32[19]{0:T(128)S(1)} %copy-done.25), kind=kOutput, calls=%fused_computation.11 | convolution fusion | flops 7159808 | bytes 1409328 | tf_op jit(solution)/shard_map/ia,axyz->ixyz/dot_general | solution.py:62
  24.8 0.9 %maximum_select_fusion = f32[2,19,4,16,128]{4,1,3,2,0:T(8,128)S(1)} fusion(f32[1,19,4,16,128]{4,1,3,2,0:T(8,128)S(1)} %fusion.10, f32[1,19,4,16,128]{4,1,3,2,0:T(8,128)S(1)} %fusion.3, pred[4,16,128]{2,1,0:T(8,128)(4,1)S(1)} %broadcast_compare_fusion, f32[2,19,4,16,128]{4,3,2,1,0:T(8,128)S(1)} %copy-done), kind=kLoop, calls=%fused_computation.2 | loop fusion | flops 622592 | bytes 3743744 | tf_op jit(solution)/shard_map/jit(_where)/select_n | solution.py:72
  26.0 2.4 %collective-permute-start.6 = (f32[2,19,1,16,128]{4,3,2,0,1:T(8,128)S(1)}, f32[2,19,1,16,128]{4,3,2,0,1:T(8,128)S(1)}, u32[]{:S(2)}, u32[]{:S(2)}) collective-permute-start(f32[2,19,1,16,128]{4,3,2,0,1:T(8,128)S(1)} %get-tuple-element.35), channel_id=1, source_target_pairs={{0,8},{8,16},{16,24},{24,0},{1,9},{9,17},{17,25},{25,1},{2,10},{10... | collective-permute-start | bytes 933896 | tf_op jit(solution)/shard_map/ppermute | solution.py:41
  28.5 0.5 collective-permute-start.7
  29.0 8.2 %collective-permute-done.6 = f32[2,19,1,16,128]{4,3,2,0,1:T(8,128)S(1)} collective-permute-done((f32[2,19,1,16,128]{4,3,2,0,1:T(8,128)S(1)}, f32[2,19,1,16,128]{4,3,2,0,1:T(8,128)S(1)}, u32[]{:S(2)}, u32[]{:S(2)}) %collective-permute-start.6) | collective-permute-done | bytes 311328 | tf_op jit(solution)/shard_map/ppermute | solution.py:41
  37.5 5.0 %collective-permute-done.7 = f32[2,19,1,16,128]{4,3,2,0,1:T(8,128)S(1)} collective-permute-done((f32[2,19,1,16,128]{4,3,2,0,1:T(8,128)S(1)}, f32[2,19,1,16,128]{4,3,2,0,1:T(8,128)S(1)}, u32[]{:S(2)}, u32[]{:S(2)}) %collective-permute-start.7) | collective-permute-done | bytes 311328 | tf_op jit(solution)/shard_map/ppermute | solution.py:44
  43.2 0.8 collective-permute-done.8
  44.7 3.4 %fusion.105 = (f32[2,19,6,18,1]{4,3,2,0,1:T(8,128)}, f32[2,19,6,18,1]{4,3,2,0,1:T(8,128)}) fusion(f32[2,19,6,18,128]{4,3,2,0,1:T(8,128)S(1)} %pad_maximum_fusion.1), kind=kLoop, calls=%fused_computation.192 | loop fusion | bytes 65664 | tf_op jit(solution)/shard_map/slice | solution.py:42
  48.1 2.9 %copy.46 = f32[2,19,6,18,1]{1,0,4,3,2:T(2,128)S(1)} copy(f32[2,19,6,18,1]{4,3,2,0,1:T(8,128)} %get-tuple-element.30) | data formatting | bytes 32832 | tf_op jit(solution)/shard_map/slice | solution.py:42
  51.0 2.9 %copy.47 = f32[2,19,6,18,1]{1,0,4,3,2:T(2,128)S(1)} copy(f32[2,19,6,18,1]{4,3,2,0,1:T(8,128)} %get-tuple-element.31) | data formatting | bytes 32832 | tf_op jit(solution)/shard_map/slice | solution.py:44
  53.9 2.2 %collective-permute-start.11 = (f32[2,19,6,18,1]{1,0,4,3,2:T(2,128)S(1)}, f32[2,19,6,18,1]{1,0,4,3,2:T(2,128)}, u32[]{:S(2)}, u32[]{:S(2)}) collective-permute-start(f32[2,19,6,18,1]{1,0,4,3,2:T(2,128)S(1)} %copy.47), channel_id=1, source_target_pairs={{1,0},{2,1},{3,2},{0,3},{5,4},{6,5},{7,6},{4,7},{9,8},{10,9},{11,1... | collective-permute-start | bytes 49256 | tf_op jit(solution)/shard_map/ppermute | solution.py:44
  56.1 0.8 %fusion.110 = (pred[4,16,128]{2,1,0:T(8,128)(4,1)S(1)}, pred[4,16,128]{2,1,0:T(8,128)(4,1)S(1)}, pred[4,16,128]{2,1,0:T(8,128)(4,1)}, pred[4,16,128]{2,1,0:T(8,1...) fusion(pred[6,18,130]{2,1,0:T(8,128)(4,1)S(1)} %fusion.11), kind=kLoop, calls=%fused_computation.197 | loop fusion | bytes 311296 | tf_op jit(solution)/shard_map/slice | solution.py:79
  57.0 5.9 %collective-permute-done.10 = f32[2,19,6,18,1]{1,0,4,3,2:T(2,128)S(1)} collective-permute-done((f32[2,19,6,18,1]{1,0,4,3,2:T(2,128)S(1)}, f32[2,19,6,18,1]{1,0,4,3,2:T(2,128)S(1)}, u32[]{:S(2)}, u32[]{:S(2)}) %collective-permute-start.10) | collective-permute-done | bytes 16448 | tf_op jit(solution)/shard_map/ppermute | solution.py:41
  62.9 3.2 %copy.48 = f32[2,19,6,18,1]{4,3,2,0,1:T(8,128)} copy(f32[2,19,6,18,1]{1,0,4,3,2:T(2,128)S(1)} %collective-permute-done.10) | data formatting | bytes 32832 | tf_op jit(solution)/shard_map/ppermute | solution.py:41
  66.1 4.1 %copy.49 = f32[2,19,6,18,1]{4,3,2,0,1:T(8,128)} copy(f32[2,19,6,18,1]{1,0,4,3,2:T(2,128)} %collective-permute-done.11) | data formatting | bytes 32832 | tf_op jit(solution)/shard_map/ppermute | solution.py:44
  70.3 6.0 %pad_maximum_fusion = f32[2,19,6,18,130]{4,3,2,0,1:T(8,128)S(1)} fusion(f32[2,19,6,18,1]{4,3,2,0,1:T(8,128)} %copy.49, f32[2,19,6,1,128]{4,3,2,0,1:T(1,128)S(1)} %collective-permute-done.9, f32[2,19,6,16,128]{4,3,2,0,1:T(8,128)S(1)} %copy-done.2, f32[2,19,6,1,128]{4,3,2,0,1:T(1,128)S(1)} %collective-permute-done.8, f32[2,19,6,18,1]{4,3,2,0,1:T(8,128)} %copy.48), kind=kLoop, calls=%fused_computation | loop fusion | flops 2134080 | bytes 4268160 | tf_op jit(solution)/shard_map/concatenate | solution.py:45
  76.3 0.6 slice_bitcast_fusion.2
  77.0 0.6 copy-done.4
  79.4 1.1 %copy.69 = f32[2,19,4,16,128]{4,3,2,1,0:T(8,128)} copy(f32[2,19,4,16,128]{4,3,2,0,1:T(8,128)S(1)} %copy_select_fusion) | data formatting | bytes 2490368 | tf_op jit(solution)/shard_map/jit(_where)/select_n | solution.py:118
  (103 shorter events, 5.9 us)
Async XLA Ops:
  0.0 2.2 %copy-start.23 = (f32[2]{0:T(128)S(1)}, f32[2]{0:T(128)}, u32[]{:S(2)}) copy-start(f32[2]{0:T(128)} %constant.14.clone) | copy-start | bytes 28
  0.0 6.4 %copy-start.22 = (f32[19,3,1,1,1]{0,1,4,3,2:T(4,128)S(1)}, f32[19,3,1,1,1]{0,1,4,3,2:T(4,128)}, u32[]{:S(2)}) copy-start(f32[19,3,1,1,1]{0,1,4,3,2:T(4,128)} %constant.40) | copy-start | bytes 688
  0.0 6.4 %copy-start = (f32[2,19,4,16,128]{4,3,2,1,0:T(8,128)S(1)}, f32[2,19,4,16,128]{4,3,2,1,0:T(8,128)}, u32[]{:S(2)}) copy-start(f32[2,19,4,16,128]{4,3,2,1,0:T(8,128)} %param.5) | copy-start | bytes 3735556
  2.4 5.7 %collective-permute-start = (f32[2,1,16,128]{3,2,1,0:T(8,128)S(1)}, f32[2,1,16,128]{3,2,1,0:T(8,128)S(1)}, u32[]{:S(2)}, u32[]{:S(2)}) collective-permute-start(f32[2,1,16,128]{3,2,1,0:T(8,128)S(1)} %get-tuple-element.49), channel_id=1, source_target_pairs={{0,8},{8,16},{16,24},{24,0},{1,9},{9,17},{17,25},{25,1},{2,10},{10... | collective-permute-start | bytes 49160 | tf_op jit(solution)/shard_map/ppermute | solution.py:41
  5.4 3.7 %collective-permute-start.1 = (f32[2,1,16,128]{3,2,1,0:T(8,128)S(1)}, f32[2,1,16,128]{3,2,1,0:T(8,128)S(1)}, u32[]{:S(2)}, u32[]{:S(2)}) collective-permute-start(f32[2,1,16,128]{3,2,1,0:T(8,128)S(1)} %get-tuple-element.50), channel_id=1, source_target_pairs={{8,0},{16,8},{24,16},{0,24},{9,1},{17,9},{25,17},{1,25},{10,2},{18... | collective-permute-start | bytes 49160 | tf_op jit(solution)/shard_map/ppermute | solution.py:44
  9.1 1.2 %collective-permute-start.2 = (f32[2,6,1,128]{3,2,1,0:T(1,128)S(1)}, f32[2,6,1,128]{3,2,1,0:T(1,128)S(1)}, u32[]{:S(2)}, u32[]{:S(2)}) collective-permute-start(f32[2,6,1,128]{3,2,1,0:T(1,128)S(1)} %get-tuple-element.40), channel_id=1, source_target_pairs={{0,4},{4,0},{1,5},{5,1},{2,6},{6,2},{3,7},{7,3},{8,12},{12,8},{9,1... | collective-permute-start | bytes 18440 | tf_op jit(solution)/shard_map/ppermute | solution.py:41
  9.2 1.3 %collective-permute-start.3 = (f32[2,6,1,128]{3,2,1,0:T(1,128)S(1)}, f32[2,6,1,128]{3,2,1,0:T(1,128)S(1)}, u32[]{:S(2)}, u32[]{:S(2)}) collective-permute-start(f32[2,6,1,128]{3,2,1,0:T(1,128)S(1)} %get-tuple-element.41), channel_id=1, source_target_pairs={{4,0},{0,4},{5,1},{1,5},{6,2},{2,6},{7,3},{3,7},{12,8},{8,12},{13,... | collective-permute-start | bytes 18440 | tf_op jit(solution)/shard_map/ppermute | solution.py:44
  10.7 8.6 %collective-permute-start.4 = (f32[2,6,18,1]{3,2,1,0:T(8,128)S(1)}, f32[2,6,18,1]{3,2,1,0:T(8,128)S(1)}, u32[]{:S(2)}, u32[]{:S(2)}) collective-permute-start(f32[2,6,18,1]{3,2,1,0:T(8,128)S(1)} %get-tuple-element.38), channel_id=1, source_target_pairs={{0,1},{1,2},{2,3},{3,0},{4,5},{5,6},{6,7},{7,4},{8,9},{9,10},{10,1... | collective-permute-start | bytes 2600 | tf_op jit(solution)/shard_map/ppermute | solution.py:41
  12.3 9.0 %collective-permute-start.5 = (f32[2,6,18,1]{3,2,1,0:T(8,128)S(1)}, f32[2,6,18,1]{3,2,1,0:T(8,128)S(1)}, u32[]{:S(2)}, u32[]{:S(2)}) collective-permute-start(f32[2,6,18,1]{3,2,1,0:T(8,128)S(1)} %get-tuple-element.39), channel_id=1, source_target_pairs={{1,0},{2,1},{3,2},{0,3},{5,4},{6,5},{7,6},{4,7},{9,8},{10,9},{11,1... | collective-permute-start | bytes 2600 | tf_op jit(solution)/shard_map/ppermute | solution.py:44
  26.0 11.5 %copy-start.3 = (f32[2,19,4,16,128]{4,3,2,0,1:T(8,128)}, f32[2,19,4,16,128]{4,3,2,0,1:T(8,128)S(1)}, u32[]{:S(2)}) copy-start(f32[2,19,4,16,128]{4,3,2,0,1:T(8,128)S(1)} %copy.43) | copy-start | bytes 3735556
  26.0 11.2 %collective-permute-start.6 = (f32[2,19,1,16,128]{4,3,2,0,1:T(8,128)S(1)}, f32[2,19,1,16,128]{4,3,2,0,1:T(8,128)S(1)}, u32[]{:S(2)}, u32[]{:S(2)}) collective-permute-start(f32[2,19,1,16,128]{4,3,2,0,1:T(8,128)S(1)} %get-tuple-element.35), channel_id=1, source_target_pairs={{0,8},{8,16},{16,24},{24,0},{1,9},{9,17},{17,25},{25,1},{2,10},{10... | collective-permute-start | bytes 933896 | tf_op jit(solution)/shard_map/ppermute | solution.py:41
  28.5 13.9 %collective-permute-start.7 = (f32[2,19,1,16,128]{4,3,2,0,1:T(8,128)S(1)}, f32[2,19,1,16,128]{4,3,2,0,1:T(8,128)S(1)}, u32[]{:S(2)}, u32[]{:S(2)}) collective-permute-start(f32[2,19,1,16,128]{4,3,2,0,1:T(8,128)S(1)} %get-tuple-element.34), channel_id=1, source_target_pairs={{8,0},{16,8},{24,16},{0,24},{9,1},{17,9},{25,17},{1,25},{10,2},{18... | collective-permute-start | bytes 933896 | tf_op jit(solution)/shard_map/ppermute | solution.py:44
  42.4 1.7 %copy-start.1 = (f32[2,19,6,16,128]{4,3,2,0,1:T(8,128)}, f32[2,19,6,16,128]{4,3,2,0,1:T(8,128)S(1)}, u32[]{:S(2)}) copy-start(f32[2,19,6,16,128]{4,3,2,0,1:T(8,128)S(1)} %constant_dynamic-update-slice_fusion) | copy-start | bytes 5603332
  42.6 1.4 %collective-permute-start.8 = (f32[2,19,6,1,128]{4,3,2,0,1:T(1,128)S(1)}, f32[2,19,6,1,128]{4,3,2,0,1:T(1,128)S(1)}, u32[]{:S(2)}, u32[]{:S(2)}) collective-permute-start(f32[2,19,6,1,128]{4,3,2,0,1:T(1,128)S(1)} %get-tuple-element.32), channel_id=1, source_target_pairs={{0,4},{4,0},{1,5},{5,1},{2,6},{6,2},{3,7},{7,3},{8,12},{12,8},{9,1... | collective-permute-start | bytes 350216 | tf_op jit(solution)/shard_map/ppermute | solution.py:41
  42.7 1.5 %collective-permute-start.9 = (f32[2,19,6,1,128]{4,3,2,0,1:T(1,128)S(1)}, f32[2,19,6,1,128]{4,3,2,0,1:T(1,128)S(1)}, u32[]{:S(2)}, u32[]{:S(2)}) collective-permute-start(f32[2,19,6,1,128]{4,3,2,0,1:T(1,128)S(1)} %get-tuple-element.33), channel_id=1, source_target_pairs={{4,0},{0,4},{5,1},{1,5},{6,2},{2,6},{7,3},{3,7},{12,8},{8,12},{13,... | collective-permute-start | bytes 350216 | tf_op jit(solution)/shard_map/ppermute | solution.py:44
  53.9 12.3 %collective-permute-start.11 = (f32[2,19,6,18,1]{1,0,4,3,2:T(2,128)S(1)}, f32[2,19,6,18,1]{1,0,4,3,2:T(2,128)}, u32[]{:S(2)}, u32[]{:S(2)}) collective-permute-start(f32[2,19,6,18,1]{1,0,4,3,2:T(2,128)S(1)} %copy.47), channel_id=1, source_target_pairs={{1,0},{2,1},{3,2},{0,3},{5,4},{6,5},{7,6},{4,7},{9,8},{10,9},{11,1... | collective-permute-start | bytes 49256 | tf_op jit(solution)/shard_map/ppermute | solution.py:44
  56.1 6.8 %collective-permute-start.10 = (f32[2,19,6,18,1]{1,0,4,3,2:T(2,128)S(1)}, f32[2,19,6,18,1]{1,0,4,3,2:T(2,128)S(1)}, u32[]{:S(2)}, u32[]{:S(2)}) collective-permute-start(f32[2,19,6,18,1]{1,0,4,3,2:T(2,128)S(1)} %copy.46), channel_id=1, source_target_pairs={{0,1},{1,2},{2,3},{3,0},{4,5},{5,6},{6,7},{7,4},{8,9},{9,10},{10,1... | collective-permute-start | bytes 49256 | tf_op jit(solution)/shard_map/ppermute | solution.py:41
  66.1 4.2 %copy-start.2 = (f32[2,19,6,16,128]{4,3,2,0,1:T(8,128)S(1)}, f32[2,19,6,16,128]{4,3,2,0,1:T(8,128)}, u32[]{:S(2)}) copy-start(f32[2,19,6,16,128]{4,3,2,0,1:T(8,128)} %copy-done.1) | copy-start | bytes 5603332
  76.3 1.3 %copy-start.4 = (f32[2,19,4,16,128]{4,3,2,0,1:T(8,128)S(1)}, f32[2,19,4,16,128]{4,3,2,0,1:T(8,128)}, u32[]{:S(2)}) copy-start(f32[2,19,4,16,128]{4,3,2,0,1:T(8,128)} %copy-done.3) | copy-start | bytes 3735556
  76.3 1.3 %copy-start.21 = (pred[4,16,128]{2,1,0:T(8,128)(4,1)S(1)}, pred[4,16,128]{2,1,0:T(8,128)(4,1)}, u32[]{:S(2)}) copy-start(pred[4,16,128]{2,1,0:T(8,128)(4,1)} %get-tuple-element.69) | copy-start | bytes 24580
  76.3 1.4 %copy-start.20 = (pred[4,16,128]{2,1,0:T(8,128)(4,1)S(1)}, pred[4,16,128]{2,1,0:T(8,128)(4,1)}, u32[]{:S(2)}) copy-start(pred[4,16,128]{2,1,0:T(8,128)(4,1)} %get-tuple-element.68) | copy-start | bytes 24580
  76.3 1.5 %copy-start.19 = (pred[4,16,128]{2,1,0:T(8,128)(4,1)S(1)}, pred[4,16,128]{2,1,0:T(8,128)(4,1)}, u32[]{:S(2)}) copy-start(pred[4,16,128]{2,1,0:T(8,128)(4,1)} %get-tuple-element.67) | copy-start | bytes 24580
  76.3 1.6 %copy-start.18 = (pred[4,16,128]{2,1,0:T(8,128)(4,1)S(1)}, pred[4,16,128]{2,1,0:T(8,128)(4,1)}, u32[]{:S(2)}) copy-start(pred[4,16,128]{2,1,0:T(8,128)(4,1)} %get-tuple-element.66) | copy-start | bytes 24580
  76.3 1.7 %copy-start.17 = (pred[4,16,128]{2,1,0:T(8,128)(4,1)S(1)}, pred[4,16,128]{2,1,0:T(8,128)(4,1)}, u32[]{:S(2)}) copy-start(pred[4,16,128]{2,1,0:T(8,128)(4,1)} %get-tuple-element.65) | copy-start | bytes 24580
  76.3 1.8 %copy-start.16 = (pred[4,16,128]{2,1,0:T(8,128)(4,1)S(1)}, pred[4,16,128]{2,1,0:T(8,128)(4,1)}, u32[]{:S(2)}) copy-start(pred[4,16,128]{2,1,0:T(8,128)(4,1)} %get-tuple-element.64) | copy-start | bytes 24580
  76.9 1.2 %copy-start.15 = (pred[4,16,128]{2,1,0:T(8,128)(4,1)S(1)}, pred[4,16,128]{2,1,0:T(8,128)(4,1)}, u32[]{:S(2)}) copy-start(pred[4,16,128]{2,1,0:T(8,128)(4,1)} %get-tuple-element.63) | copy-start | bytes 24580
  77.0 1.3 %copy-start.14 = (pred[4,16,128]{2,1,0:T(8,128)(4,1)S(1)}, pred[4,16,128]{2,1,0:T(8,128)(4,1)}, u32[]{:S(2)}) copy-start(pred[4,16,128]{2,1,0:T(8,128)(4,1)} %get-tuple-element.62) | copy-start | bytes 24580
  77.0 1.4 %copy-start.13 = (pred[4,16,128]{2,1,0:T(8,128)(4,1)S(1)}, pred[4,16,128]{2,1,0:T(8,128)(4,1)}, u32[]{:S(2)}) copy-start(pred[4,16,128]{2,1,0:T(8,128)(4,1)} %get-tuple-element.61) | copy-start | bytes 24580
  77.0 1.5 %copy-start.12 = (pred[4,16,128]{2,1,0:T(8,128)(4,1)S(1)}, pred[4,16,128]{2,1,0:T(8,128)(4,1)}, u32[]{:S(2)}) copy-start(pred[4,16,128]{2,1,0:T(8,128)(4,1)} %get-tuple-element.60) | copy-start | bytes 24580
  77.0 1.6 %copy-start.11 = (pred[4,16,128]{2,1,0:T(8,128)(4,1)S(1)}, pred[4,16,128]{2,1,0:T(8,128)(4,1)}, u32[]{:S(2)}) copy-start(pred[4,16,128]{2,1,0:T(8,128)(4,1)} %get-tuple-element.59) | copy-start | bytes 24580
  77.0 1.7 %copy-start.10 = (pred[4,16,128]{2,1,0:T(8,128)(4,1)S(1)}, pred[4,16,128]{2,1,0:T(8,128)(4,1)}, u32[]{:S(2)}) copy-start(pred[4,16,128]{2,1,0:T(8,128)(4,1)} %get-tuple-element.58) | copy-start | bytes 24580
  77.6 1.1 %copy-start.9 = (pred[4,16,128]{2,1,0:T(8,128)(4,1)S(1)}, pred[4,16,128]{2,1,0:T(8,128)(4,1)}, u32[]{:S(2)}) copy-start(pred[4,16,128]{2,1,0:T(8,128)(4,1)} %get-tuple-element.57) | copy-start | bytes 24580
  (6 other events, 5.6 us)
where the time goes:
time: 80.7 us; the launch traced here: 80.5 us
  waiting for transfers between devices  27.9 us (35%)
  local copies, waits for them, and re-layouts  21.3 us (26%)
  starting transfers between devices  14.3 us (18%)
  other arithmetic  12.5 us (15%)
  matrix products  3.77 us (5%)
    ppermute x6, waiting for transfers between devices, extended(): lax.ppermute(lax.slice_in_dim(block, block.shape[dim] - width, None, axis...  19.6 us
    ppermute x6, waiting for transfers between devices, extended(): lax.ppermute(lax.slice_in_dim(block, 0, width, axis=dim), axis, backward)  8.34 us
    ppermute x6, starting transfers between devices, extended(): lax.ppermute(lax.slice_in_dim(block, block.shape[dim] - width, None, axis...  7.24 us
    ppermute x6, starting transfers between devices, extended(): lax.ppermute(lax.slice_in_dim(block, 0, width, axis=dim), axis, backward)  7.01 us
    slice x5, local copies, waits for them, and re-layouts, extended(): lax.slice_in_dim(block, block.shape[dim] - width, None, axis=dim)  6.56 us
    concatenate x3, other arithmetic, extended(): block = jnp.concatenate([low, block, high], axis=dim)  6.5 us
    ppermute x1, local copies, waits for them, and re-layouts, extended(): lax.ppermute(lax.slice_in_dim(block, 0, width, axis=dim), axis, backward)  4.15 us
    ppermute x1, local copies, waits for them, and re-layouts, extended(): lax.ppermute(lax.slice_in_dim(block, block.shape[dim] - width, None, axis...  3.21 us
  transfers between devices with their start and end apart: 12, of which 10 were waited for; matrix products, arithmetic and copies ran while one was open for 8% of the time, Pallas kernels for 0%

commit v1 on v0

v1 whole, which is shorter than its diff:
```python
import jax
import jax.numpy as jnp
from jax import lax
from jax.experimental import pallas as pl
from jax.experimental.pallas import tpu as pltpu
from jax.sharding import PartitionSpec as P

VELOCITIES = [
    (0, 0, 0),
    (1, 0, 0),
    (-1, 0, 0),
    (0, 1, 0),
    (0, -1, 0),
    (0, 0, 1),
    (0, 0, -1),
    (1, 1, 0),
    (-1, -1, 0),
    (1, -1, 0),
    (-1, 1, 0),
    (1, 0, 1),
    (-1, 0, -1),
    (1, 0, -1),
    (-1, 0, 1),
    (0, 1, 1),
    (0, -1, -1),
    (0, 1, -1),
    (0, -1, 1),
]
WEIGHTS = [1.0 / 3.0] + [1.0 / 18.0] * 6 + [1.0 / 36.0] * 12
OPPOSITE = [0, 2, 1, 4, 3, 6, 5, 8, 7, 10, 9, 12, 11, 14, 13, 16, 15, 18, 17]
COUPLING = 0.9
RELAX = (1.0, 0.8)
WALL = (0.3, 1.5)
AXES = ("gx", "gy", "gz")
MESH = pl.DeviceIdType.MESH

ORDER = (
    [0]
    + [i for i in range(19) if VELOCITIES[i][0] == 1]
    + [i for i in range(19) if VELOCITIES[i][0] == -1]
    + [i for i in range(1, 19) if VELOCITIES[i][0] == 0]
)
SLOT = {i: s for s, i in enumerate(ORDER)}
Z_UP = [i for i in range(19) if VELOCITIES[i][2] == 1]
Z_PAIR = {}
for _g, _i in enumerate(Z_UP):
    Z_PAIR[_i] = _g
    Z_PAIR[OPPOSITE[_i]] = _g
Z_OFFSETS = [v for v in VELOCITIES if v[2] != 0]
Z_INDEX = {v: n for n, v in enumerate(Z_OFFSETS)}
T = 8
LANES = 128


def step_kernel(pop_hbm, solid_hbm, out_hbm, pop, solid, out, psi, zpsi, post, zpost, vel, source,
                pack1, recv1, pack2, recv2, load_sem, store_sem, send1, got1, send2, got2):
    X, Y, Z = solid.shape
    YT = Y // T
    lo, hi = slice(T, 2 * T), slice(Y, Y + T)
    low_halo, high_halo = slice(0, T), slice(Y + T, Y + 2 * T)
    inner = slice(T, Y + T)

    loads = [pltpu.make_async_copy(solid_hbm, solid, load_sem.at[X])]
    loads += [
        pltpu.make_async_copy(pop_hbm.at[:, :, x], pop.at[:, :, x], load_sem.at[x])
        for x in range(X)
    ]
    for copy in loads:
        copy.start()

    me = [lax.axis_index(a) for a in AXES]
    count = [lax.axis_size(a) for a in AXES]

    def device(offset):
        return tuple(lax.rem(me[d] + offset[d] + count[d], count[d]) for d in range(3))

    barrier = pltpu.get_barrier_semaphore()
    for offset in VELOCITIES[1:]:
        pl.semaphore_signal(barrier, inc=1, device_id=device(offset), device_id_type=MESH)

    lane = lax.broadcasted_iota(jnp.int32, (T, LANES), 1)
    pair = lane // 2
    lane_y = lax.broadcasted_iota(jnp.int32, (Y, LANES), 1)
    first, last = lane_y == 0, lane_y == Z - 1

    loads[0].wait()
    inv = [1.0 / t for t in RELAX]
    packed = jnp.zeros((T, LANES), jnp.float32)

    def combo1(k, x, t):
        return (k * X + x) * YT + t

    for x in range(X):
        loads[1 + x].wait()
        fluid = solid[x] == 0
        total, mom = [], [[], [], []]
        for k in range(2):
            f = [pop[k, i, x] for i in range(19)]
            rho = f[0]
            m = [None, None, None]
            for i in range(1, 19, 2):
                rho = rho + (f[i] + f[i + 1])
                diff = f[i] - f[i + 1]
                for d in range(3):
                    c = VELOCITIES[i][d]
                    if c:
                        m[d] = (
                            (diff if c > 0 else -diff)
                            if m[d] is None
                            else (m[d] + diff if c > 0 else m[d] - diff)
                        )
            total.append(rho)
            signed = jnp.where(fluid, rho, -WALL[k])
            psi[k, 1 + x, inner] = signed
            for d in range(3):
                mom[d].append(m[d] * inv[k] if inv[k] != 1.0 else m[d])
            for t in range(YT):
                j = combo1(k, x, t)
                piece = pltpu.roll(signed[t * T:(t + 1) * T], (2 * j + 1) % LANES, 1)
                packed = jnp.where(pair == j, piece, packed)
        scale = 1.0 / (total[0] * inv[0] + total[1] * inv[1])
        for d in range(3):
            vel[d, x] = (mom[d][0] + mom[d][1]) * scale
    pack1[...] = packed

    pl.semaphore_wait(barrier, 18)

    def remote(src, dst, send, recv, n, offset):
        return pltpu.make_async_remote_copy(
            src_ref=src,
            dst_ref=dst,
            send_sem=send.at[n],
            recv_sem=recv.at[n],
            device_id=device(offset),
            device_id_type=MESH,
        )

    def edge_of(offset):
        dx, dy, _ = offset
        src_x = slice(1, X + 1) if dx == 0 else (slice(X, X + 1) if dx > 0 else slice(1, 2))
        dst_x = slice(1, X + 1) if dx == 0 else (slice(0, 1) if dx > 0 else slice(X + 1, X + 2))
        src_y = inner if dy == 0 else (hi if dy > 0 else lo)
        dst_y = inner if dy == 0 else (low_halo if dy > 0 else high_halo)
        return (src_x, src_y), (dst_x, dst_y)

    order = sorted(range(1, 19), key=lambda i: -sum(abs(c) for c in VELOCITIES[i][::2]))
    copies1 = []
    for n, i in enumerate(order):
        offset = VELOCITIES[i]
        if offset[2]:
            copy = remote(pack1, recv1.at[Z_INDEX[offset]], send1, got1, n, offset)
        else:
            s, d = edge_of(offset)
            copy = remote(psi.at[:, s[0], s[1]], psi.at[:, d[0], d[1]], send1, got1, n, offset)
        copy.start()
        copies1.append(copy)
    for copy in copies1:
        copy.wait_recv()

    def came1(x, y, z):
        return recv1[Z_INDEX[(-x, -y, -z)]]

    def put1(merged, k, x, t, plane, rows):
        zpsi[k, plane, rows] = pltpu.roll(merged, (LANES - 2 * combo1(k, x, t) - 1) % LANES, 1)

    even = lane % 2 == 0
    for dx, dy in ((0, 0), (-1, 0), (1, 0), (0, -1), (0, 1)):
        merged = jnp.where(even, came1(dx, dy, -1), came1(dx, dy, 1))
        xs = range(X) if dx == 0 else ([X - 1] if dx < 0 else [0])
        ts = range(YT) if dy == 0 else ([YT - 1] if dy < 0 else [0])
        for k in range(2):
            for x in xs:
                for t in ts:
                    plane = 1 + x + dx * X
                    row = T * (1 + t + dy * YT)
                    put1(merged, k, x, t, plane, slice(row, row + T))

    def shifted(base, edge, move):
        if move[2] == 0:
            return base
        if move[2] > 0:
            return pltpu.roll(jnp.where(first, edge, base), Z - 1, 1)
        return pltpu.roll(jnp.where(last, edge, base), 1, 1)

    half = X // 2

    def combo2(k, g, x, t):
        return (((x % half) * 2 + k) * 5 + g) * YT + t

    packs = [jnp.zeros((T, LANES), jnp.float32) for _ in range(2)]
    for x in range(X):
        grads = []
        for k in range(2):
            parts = [None, None, None]
            beside = {}
            for i in range(1, 19):
                c = VELOCITIES[i]
                at = (k, 1 + x + c[0], slice(T + c[1], T + c[1] + Y))
                value = shifted(psi[at], zpsi[at] if c[2] else None, c)
                if k == 0:
                    source[OPPOSITE[i], x] = value
                beside[i] = jnp.abs(value)
            for i in range(1, 19, 2):
                term = WEIGHTS[i] * (beside[i] - beside[i + 1])
                for d in range(3):
                    c = VELOCITIES[i][d]
                    if c:
                        parts[d] = (
                            (term if c > 0 else -term)
                            if parts[d] is None
                            else (parts[d] + term if c > 0 else parts[d] - term)
                        )
            grads.append(parts)
        for k in range(2):
            u = [vel[d, x] - (COUPLING * RELAX[k]) * grads[1 - k][d] for d in range(3)]
            rho = jnp.abs(psi[k, 1 + x, inner]) * inv[k]
            rest = 1.0 - inv[k]
            flat = 1.0 - 1.5 * (u[0] * u[0] + u[1] * u[1] + u[2] * u[2])
            keep = 1.0 - inv[k]
            rho_w = {w: rho * w for w in set(WEIGHTS)}
            values = {}

            def finish(i, eq):
                if abs(keep) > 1e-9:
                    eq = eq + keep * pop[k, i, x]
                post[k, SLOT[i], 1 + x, inner] = eq
                values[i] = eq

            finish(0, rho_w[WEIGHTS[0]] * flat)
            for i in range(1, 19, 2):
                along = None
                for d in range(3):
                    c = VELOCITIES[i][d]
                    if c:
                        along = (
                            (u[d] if c > 0 else -u[d])
                            if along is None
                            else (along + u[d] if c > 0 else along - u[d])
                        )
                w = rho_w[WEIGHTS[i]]
                even_part = w * (flat + 4.5 * (along * along))
                odd_part = w * (3.0 * along)
                finish(i, even_part + odd_part)
                finish(i + 1, even_part - odd_part)
            for g, i in enumerate(Z_UP):
                ends = jnp.where(last, values[i], values[OPPOSITE[i]])
                for t in range(YT):
                    j = combo2(k, g, x, t)
                    piece = pltpu.roll(ends[t * T:(t + 1) * T], (2 * j + 1) % LANES, 1)
                    packs[x // half] = jnp.where(pair == j, piece, packs[x // half])
    for h in range(2):
        pack2[h] = packs[h]

    copies2 = []

    def launch2(src, dst, offset):
        copy = remote(src, dst, send2, got2, len(copies2), offset)
        copy.start()
        copies2.append(copy)

    for i in order:
        offset = VELOCITIES[i]
        if offset[2]:
            halves = slice(0, 2) if offset[0] == 0 else (slice(1, 2) if offset[0] > 0 else slice(0, 1))
            launch2(pack2.at[halves], recv2.at[Z_INDEX[offset], halves], offset)
            continue
        s, d = edge_of(offset)
        if offset[0] and offset[1]:
            launch2(post.at[:, SLOT[i], s[0], s[1]], post.at[:, SLOT[i], d[0], d[1]], offset)
        elif offset[0]:
            group = slice(1, 6) if offset[0] > 0 else slice(6, 11)
            launch2(post.at[:, group, s[0], s[1]], post.at[:, group, d[0], d[1]], offset)
        else:
            for q in range(19):
                if VELOCITIES[q][1] == offset[1]:
                    launch2(post.at[:, SLOT[q], s[0], s[1]], post.at[:, SLOT[q], d[0], d[1]], offset)

    for x in range(X):
        fluid = solid[x] == 0
        for k in range(2):
            out[k, 0, x] = jnp.where(fluid, post[k, 0, 1 + x, inner], pop[k, 0, x])

    for copy in copies2:
        copy.wait_recv()

    def came2(x, y, z, h):
        return recv2[Z_INDEX[(-x, -y, -z)], h]

    def put2(tile, k, g, x, t, plane, rows):
        zpost[k, g, plane, rows] = pltpu.roll(tile, (LANES - 2 * combo2(k, g, x, t) - 1) % LANES, 1)

    for h in range(2):
        merged = jnp.where(even, came2(0, 0, -1, h), came2(0, 0, 1, h))
        for x in range(h * half, (h + 1) * half):
            for k in range(2):
                for g in range(5):
                    for t in range(YT):
                        row = T * (1 + t)
                        put2(merged, k, g, x, t, 1 + x, slice(row, row + T))
    for i in range(1, 19):
        c = VELOCITIES[i]
        if c[2] == 0 or (c[0] == 0 and c[1] == 0):
            continue
        g = Z_PAIR[i]
        for k in range(2):
            if c[0]:
                x = X - 1 if c[0] > 0 else 0
                plane = 0 if c[0] > 0 else X + 1
                for t in range(YT):
                    row = T * (1 + t)
                    put2(came2(-c[0], 0, -c[2], x // half), k, g, x, t, plane, slice(row, row + T))
            else:
                t = YT - 1 if c[1] > 0 else 0
                rows = low_halo if c[1] > 0 else high_halo
                for x in range(X):
                    put2(came2(0, -c[1], -c[2], x // half), k, g, x, t, 1 + x, rows)

    stores = []
    for x in range(X):
        fluid = solid[x] == 0
        for k in range(2):
            for i in range(1, 19):
                c = VELOCITIES[i]
                back = tuple(-a for a in c)
                rows = slice(T - c[1], T - c[1] + Y)
                base = post[k, SLOT[i], 1 + x - c[0], rows]
                edge = zpost[k, Z_PAIR[i], 1 + x - c[0], rows] if c[2] else None
                pulled = shifted(base, edge, back)
                bounced = post[k, SLOT[OPPOSITE[i]], 1 + x, inner]
                read = jnp.where(source[i, x] > 0.0, pulled, bounced)
                out[k, i, x] = jnp.where(fluid, read, pop[k, i, x])
        copy = pltpu.make_async_copy(out.at[:, :, x], out_hbm.at[:, :, x], store_sem.at[x])
        copy.start()
        stores.append(copy)
    for copy in copies1 + copies2:
        copy.wait_send()
    for copy in stores:
        copy.wait()


def body(populations, solid):
    X, Y, Z = solid.shape
    f32 = jnp.float32
    dma = pltpu.SemaphoreType.DMA
    return pl.pallas_call(
        step_kernel,
        out_shape=jax.ShapeDtypeStruct(populations.shape, f32),
        in_specs=[pl.BlockSpec(memory_space=pl.ANY)] * 2,
        out_specs=pl.BlockSpec(memory_space=pl.ANY),
        scratch_shapes=[
            pltpu.VMEM(populations.shape, f32),
            pltpu.VMEM(solid.shape, jnp.int32),
            pltpu.VMEM(populations.shape, f32),
            pltpu.VMEM((2, X + 2, Y + 2 * T, Z), f32),
            pltpu.VMEM((2, X + 2, Y + 2 * T, Z), f32),
            pltpu.VMEM((2, 19, X + 2, Y + 2 * T, Z), f32),
            pltpu.VMEM((2, 5, X + 2, Y + 2 * T, Z), f32),
            pltpu.VMEM((3, X, Y, Z), f32),
            pltpu.VMEM((19, X, Y, Z), f32),
            pltpu.VMEM((T, LANES), f32),
            pltpu.VMEM((10, T, LANES), f32),
            pltpu.VMEM((2, T, LANES), f32),
            pltpu.VMEM((10, 2, T, LANES), f32),
            dma((X + 1,)),
            dma((X,)),
            dma((18,)),
            dma((18,)),
            dma((26,)),
            dma((26,)),
        ],
        compiler_params=pltpu.CompilerParams(collective_id=0, has_side_effects=True),
    )(populations, solid)


def solution(mesh):
    in_specs = (P(None, None, "gx", "gy", "gz"), P("gx", "gy", "gz"))
    out_specs = P(None, None, "gx", "gy", "gz")
    return jax.shard_map(body, mesh=mesh, in_specs=in_specs, out_specs=out_specs, check_vma=False)
```

time: 80.7 us -> 22.2 us (0.28)
  waiting for transfers between devices: 27.9 us -> 0 us
  Pallas kernels: 0 us -> 19.6 us
  local copies, waits for them, and re-layouts: 21.3 us -> 2.47 us
  starting transfers between devices: 14.3 us -> 0 us
  other arithmetic: 12.5 us -> 0 us
  matrix products: 3.77 us -> 0 us
    ppermute x12 -> x0, waiting for transfers between devices: 27.9 us -> none  [the longest x6 19.6 us: extended(): lax.ppermute(lax.slice_in_dim(block, block.shape[dim] - width, None, axis...]
    pallas_call x0 -> x1, Pallas kernels: none -> 19.6 us  [body(): pl.pallas_call(step_kernel, out_shape=jax.ShapeDtypeStruct(populations.sh...]
    ppermute x12 -> x0, starting transfers between devices: 14.3 us -> none  [the longest x6 7.24 us: extended(): lax.ppermute(lax.slice_in_dim(block, block.shape[dim] - width, None, axis...]
    slice x9 -> x0, local copies, waits for them, and re-layouts: 10.4 us -> none  [the longest x5 6.56 us: extended(): lax.slice_in_dim(block, block.shape[dim] - width, None, axis=dim)]
    ppermute x2 -> x0, local copies, waits for them, and re-layouts: 7.36 us -> none  [the longest x1 4.15 us: extended(): lax.ppermute(lax.slice_in_dim(block, 0, width, axis=dim), axis, backward)]
    concatenate x3 -> x0, other arithmetic: 6.5 us -> none  [extended(): block = jnp.concatenate([low, block, high], axis=dim)]
    dot_general x3 -> x0, matrix products: 3.77 us -> none  [the longest x2 2.16 us: collide(): jnp.einsum('ia,axyz->ixyz', vel, velocity, precision=lax.Precision.HIGHEST)]
    reduce_sum x2 -> x0, other arithmetic: 1.67 us -> none  [the longest x1 1.37 us: body(): rho = jnp.sum(populations, axis=1)]
  transfers between devices with their start and end apart: 12 -> 0, of which waited for: 10 -> 0; matrix products, arithmetic and copies ran while one was open for 8% -> 0% of each run, Pallas kernels for 0% -> 0%
where the time goes in v1:
time: 22.2 us; the launch traced here: 22.1 us
  Pallas kernels  19.6 us (88%)
  local copies, waits for them, and re-layouts  2.47 us (11%)
    pallas_call x1, Pallas kernels, body(): pl.pallas_call(step_kernel, out_shape=jax.ShapeDtypeStruct(populations.sh...  19.6 us
    unnamed x1, local copies, waits for them, and re-layouts  2.47 us

profile of v1, /device:TPU:0, one launch (start us, length us, event | category | flops | bytes accessed | tf_op | source)
XLA Modules:
  0.0 22.1 jit_solution(2534008836235876632)
XLA Ops:
  0.0 19.6 %shard_map.28 = f32[2,19,4,16,128]{4,3,2,1,0:T(8,128)} custom-call(f32[2,19,4,16,128]{4,3,2,1,0:T(8,128)} %pop_hbm.1, s32[4,16,128]{2,1,0:T(8,128)} %solid_hbm.1), custom_call_target="tpu_custom_call" | custom-call | tf_op jit(solution)/shard_map/pallas_call | solution.py:345
  19.6 2.5 %copy.4 = f32[2,19,4,16,128]{4,3,2,1,0:T(8,128)} copy(f32[2,19,4,16,128]{4,3,2,1,0:T(8,128)} %shard_map.28) | data formatting | bytes 2490368

commit v2 on v1

--- a/solution.py
+++ b/solution.py
@@ -52,8 +52,8 @@
 LANES = 128
 
 
-def step_kernel(pop_hbm, solid_hbm, out_hbm, pop, solid, out, psi, zpsi, post, zpost, vel, source,
-                pack1, recv1, pack2, recv2, load_sem, store_sem, send1, got1, send2, got2):
+def step_kernel(pop_hbm, solid_hbm, out, pop, solid, psi, zpsi, post, zpost, vel, source,
+                pack1, recv1, pack2, recv2, face, ghost, load_sem, send1, got1, send2, got2):
     X, Y, Z = solid.shape
     YT = Y // T
     lo, hi = slice(T, 2 * T), slice(Y, Y + T)
@@ -75,7 +75,8 @@
         return tuple(lax.rem(me[d] + offset[d] + count[d], count[d]) for d in range(3))
 
     barrier = pltpu.get_barrier_semaphore()
-    for offset in VELOCITIES[1:]:
+    greeted = [v for v in VELOCITIES[1:] if not (v[0] and v[2])]
+    for offset in greeted:
         pl.semaphore_signal(barrier, inc=1, device_id=device(offset), device_id_type=MESH)
 
     lane = lax.broadcasted_iota(jnp.int32, (T, LANES), 1)
@@ -123,7 +124,7 @@
             vel[d, x] = (mom[d][0] + mom[d][1]) * scale
     pack1[...] = packed
 
-    pl.semaphore_wait(barrier, 18)
+    pl.semaphore_wait(barrier, len(greeted))
 
     def remote(src, dst, send, recv, n, offset):
         return pltpu.make_async_remote_copy(
@@ -144,18 +145,35 @@
         return (src_x, src_y), (dst_x, dst_y)
 
     order = sorted(range(1, 19), key=lambda i: -sum(abs(c) for c in VELOCITIES[i][::2]))
-    copies1 = []
-    for n, i in enumerate(order):
-        offset = VELOCITIES[i]
+    copies1 = {}
+    for offset in sorted(greeted, key=lambda v: (-abs(v[2]), abs(v[0]) + abs(v[1]))):
+        n = len(copies1)
         if offset[2]:
             copy = remote(pack1, recv1.at[Z_INDEX[offset]], send1, got1, n, offset)
         else:
             s, d = edge_of(offset)
             copy = remote(psi.at[:, s[0], s[1]], psi.at[:, d[0], d[1]], send1, got1, n, offset)
         copy.start()
-        copies1.append(copy)
-    for copy in copies1:
-        copy.wait_recv()
+        copies1[offset] = copy
+    raw = []
+    for side in (1, -1):
+        for i in range(19):
+            if VELOCITIES[i][0] == side:
+                src_plane, dst_plane = (X - 1, 0) if side > 0 else (0, X + 1)
+                copy = remote(pop.at[1, i, src_plane], post.at[1, SLOT[i], dst_plane, inner],
+                              send1, got1, 18 + len(raw), (side, 0, 0))
+                copy.start()
+                raw.append(copy)
+    for dz in (1, -1):
+        copies1[(0, 0, dz)].wait_recv()
+        for dx in (1, -1):
+            copy = remote(recv1.at[Z_INDEX[(0, 0, dz)]], recv1.at[Z_INDEX[(dx, 0, dz)]],
+                          send1, got1, len(copies1), (dx, 0, 0))
+            copy.start()
+            copies1[(dx, 0, dz)] = copy
+    for offset in greeted:
+        if offset[:2] != (0, 0):
+            copies1[offset].wait_recv()
 
     def came1(x, y, z):
         return recv1[Z_INDEX[(-x, -y, -z)]]
@@ -164,7 +182,8 @@
         zpsi[k, plane, rows] = pltpu.roll(merged, (LANES - 2 * combo1(k, x, t) - 1) % LANES, 1)
 
     even = lane % 2 == 0
-    for dx, dy in ((0, 0), (-1, 0), (1, 0), (0, -1), (0, 1)):
+
+    def unpack1(dx, dy):
         merged = jnp.where(even, came1(dx, dy, -1), came1(dx, dy, 1))
         xs = range(X) if dx == 0 else ([X - 1] if dx < 0 else [0])
         ts = range(YT) if dy == 0 else ([YT - 1] if dy < 0 else [0])
@@ -174,6 +193,9 @@
                     plane = 1 + x + dx * X
                     row = T * (1 + t + dy * YT)
                     put1(merged, k, x, t, plane, slice(row, row + T))
+
+    for dx, dy in ((0, 0), (0, -1), (0, 1)):
+        unpack1(dx, dy)
 
     def shifted(base, edge, move):
         if move[2] == 0:
@@ -187,8 +209,49 @@
     def combo2(k, g, x, t):
         return (((x % half) * 2 + k) * 5 + g) * YT + t
 
+    def equilibrium(pairs, rho_of, u):
+        flat = 1.0 - 1.5 * (u[0] * u[0] + u[1] * u[1] + u[2] * u[2])
+        result = {}
+        for i, signs in pairs:
+            if i == 0:
+                result[0] = rho_of[WEIGHTS[0]] * flat
+                continue
+            along = None
+            for d in range(3):
+                c = VELOCITIES[i][d]
+                if c:
+                    along = (
+                        (u[d] if c > 0 else -u[d])
+                        if along is None
+                        else (along + u[d] if c > 0 else along - u[d])
+                    )
+            w = rho_of[WEIGHTS[i]]
+            even_part = w * (flat + 4.5 * (along * along))
+            odd_part = w * (3.0 * along)
+            if 1 in signs:
+                result[i] = even_part + odd_part
+            if -1 in signs:
+                result[i + 1] = even_part - odd_part
+        return result
+
+    everything = [(0, (1,))] + [(i, (1, -1)) for i in range(1, 19, 2)]
+    copies2 = []
+    kinds = []
+
+    def launch2(src, dst, offset):
+        copy = remote(src, dst, send2, got2, len(copies2), offset)
+        copy.start()
+        copies2.append(copy)
+        kinds.append(tuple(abs(c) for c in offset))
+
     packs = [jnp.zeros((T, LANES), jnp.float32) for _ in range(2)]
-    for x in range(X):
+    for x in list(range(1, X - 1)) + [0, X - 1]:
+        if x == 0:
+            for dx in (1, -1):
+                for dz in (1, -1):
+                    copies1[(dx, 0, dz)].wait_recv()
+            for dx in (1, -1):
+                unpack1(dx, 0)
         grads = []
         for k in range(2):
             parts = [None, None, None]
@@ -214,49 +277,26 @@
         for k in range(2):
             u = [vel[d, x] - (COUPLING * RELAX[k]) * grads[1 - k][d] for d in range(3)]
             rho = jnp.abs(psi[k, 1 + x, inner]) * inv[k]
-            rest = 1.0 - inv[k]
-            flat = 1.0 - 1.5 * (u[0] * u[0] + u[1] * u[1] + u[2] * u[2])
             keep = 1.0 - inv[k]
-            rho_w = {w: rho * w for w in set(WEIGHTS)}
-            values = {}
-
-            def finish(i, eq):
+            values = equilibrium(everything, {w: rho * w for w in sorted(set(WEIGHTS))}, u)
+            for i in range(19):
                 if abs(keep) > 1e-9:
-                    eq = eq + keep * pop[k, i, x]
-                post[k, SLOT[i], 1 + x, inner] = eq
-                values[i] = eq
-
-            finish(0, rho_w[WEIGHTS[0]] * flat)
-            for i in range(1, 19, 2):
-                along = None
+                    values[i] = values[i] + keep * pop[k, i, x]
+                post[k, SLOT[i], 1 + x, inner] = values[i]
+            if x in (0, X - 1):
                 for d in range(3):
-                    c = VELOCITIES[i][d]
-                    if c:
-                        along = (
-                            (u[d] if c > 0 else -u[d])
-                            if along is None
-                            else (along + u[d] if c > 0 else along - u[d])
-                        )
-                w = rho_w[WEIGHTS[i]]
-                even_part = w * (flat + 4.5 * (along * along))
-                odd_part = w * (3.0 * along)
-                finish(i, even_part + odd_part)
-                finish(i + 1, even_part - odd_part)
+                    face[int(x != 0), 3 * k + d] = u[d]
             for g, i in enumerate(Z_UP):
                 ends = jnp.where(last, values[i], values[OPPOSITE[i]])
                 for t in range(YT):
                     j = combo2(k, g, x, t)
                     piece = pltpu.roll(ends[t * T:(t + 1) * T], (2 * j + 1) % LANES, 1)
                     packs[x // half] = jnp.where(pair == j, piece, packs[x // half])
+        if x in (0, X - 1):
+            side = int(x != 0)
+            launch2(face.at[side], ghost.at[1 - side], (2 * side - 1, 0, 0))
     for h in range(2):
         pack2[h] = packs[h]
-
-    copies2 = []
-
-    def launch2(src, dst, offset):
-        copy = remote(src, dst, send2, got2, len(copies2), offset)
-        copy.start()
-        copies2.append(copy)
 
     for i in order:
         offset = VELOCITIES[i]
@@ -267,21 +307,60 @@
         s, d = edge_of(offset)
         if offset[0] and offset[1]:
             launch2(post.at[:, SLOT[i], s[0], s[1]], post.at[:, SLOT[i], d[0], d[1]], offset)
-        elif offset[0]:
-            group = slice(1, 6) if offset[0] > 0 else slice(6, 11)
-            launch2(post.at[:, group, s[0], s[1]], post.at[:, group, d[0], d[1]], offset)
-        else:
+        elif offset[1]:
             for q in range(19):
                 if VELOCITIES[q][1] == offset[1]:
                     launch2(post.at[:, SLOT[q], s[0], s[1]], post.at[:, SLOT[q], d[0], d[1]], offset)
 
-    for x in range(X):
+    def await2(*wanted):
+        for copy, kind in zip(copies2, kinds):
+            if kind in wanted:
+                copy.wait_recv()
+
+    def stream(x, still_z):
         fluid = solid[x] == 0
         for k in range(2):
-            out[k, 0, x] = jnp.where(fluid, post[k, 0, 1 + x, inner], pop[k, 0, x])
-
-    for copy in copies2:
+            for i in range(19):
+                c = VELOCITIES[i]
+                if (c[2] == 0) != still_z:
+                    continue
+                rows = slice(T - c[1], T - c[1] + Y)
+                read = post[k, SLOT[i], 1 + x - c[0], rows]
+                if i:
+                    edge = zpost[k, Z_PAIR[i], 1 + x - c[0], rows] if c[2] else None
+                    read = shifted(read, edge, tuple(-a for a in c))
+                    bounced = post[k, SLOT[OPPOSITE[i]], 1 + x, inner]
+                    read = jnp.where(source[i, x] > 0.0, read, bounced)
+                out[k, i, x] = jnp.where(fluid, read, pop[k, i, x])
+
+    await2((0, 1, 0))
+    for x in range(1, X - 1):
+        stream(x, True)
+
+    for copy in raw:
         copy.wait_recv()
+    await2((1, 0, 0))
+    for side in range(2):
+        plane = 0 if side == 0 else X + 1
+        sign = 1 if side == 0 else -1
+        wanted = []
+        for i in range(1, 19, 2):
+            if VELOCITIES[i][0]:
+                wanted.append((i, (sign * VELOCITIES[i][0],)))
+        for k in range(2):
+            rho = jnp.abs(psi[k, plane, inner]) * inv[k]
+            u = [ghost[side, 3 * k + d] for d in range(3)]
+            keep = 1.0 - inv[k]
+            values = equilibrium(wanted, {w: rho * w for w in sorted(set(WEIGHTS))}, u)
+            for i in values:
+                value = values[i]
+                if abs(keep) > 1e-9:
+                    value = value + keep * post[k, SLOT[i], plane, inner]
+                post[k, SLOT[i], plane, inner] = value
+    await2((1, 1, 0))
+    for x in (0, X - 1):
+        stream(x, True)
+    await2((0, 0, 1), (0, 1, 1))
 
     def came2(x, y, z, h):
         return recv2[Z_INDEX[(-x, -y, -z)], h]
@@ -297,45 +376,34 @@
                     for t in range(YT):
                         row = T * (1 + t)
                         put2(merged, k, g, x, t, 1 + x, slice(row, row + T))
-    for i in range(1, 19):
-        c = VELOCITIES[i]
-        if c[2] == 0 or (c[0] == 0 and c[1] == 0):
-            continue
-        g = Z_PAIR[i]
-        for k in range(2):
-            if c[0]:
-                x = X - 1 if c[0] > 0 else 0
-                plane = 0 if c[0] > 0 else X + 1
-                for t in range(YT):
-                    row = T * (1 + t)
-                    put2(came2(-c[0], 0, -c[2], x // half), k, g, x, t, plane, slice(row, row + T))
-            else:
-                t = YT - 1 if c[1] > 0 else 0
-                rows = low_halo if c[1] > 0 else high_halo
-                for x in range(X):
-                    put2(came2(0, -c[1], -c[2], x // half), k, g, x, t, 1 + x, rows)
-
-    stores = []
-    for x in range(X):
-        fluid = solid[x] == 0
-        for k in range(2):
-            for i in range(1, 19):
-                c = VELOCITIES[i]
-                back = tuple(-a for a in c)
-                rows = slice(T - c[1], T - c[1] + Y)
-                base = post[k, SLOT[i], 1 + x - c[0], rows]
-                edge = zpost[k, Z_PAIR[i], 1 + x - c[0], rows] if c[2] else None
-                pulled = shifted(base, edge, back)
-                bounced = post[k, SLOT[OPPOSITE[i]], 1 + x, inner]
-                read = jnp.where(source[i, x] > 0.0, pulled, bounced)
-                out[k, i, x] = jnp.where(fluid, read, pop[k, i, x])
-        copy = pltpu.make_async_copy(out.at[:, :, x], out_hbm.at[:, :, x], store_sem.at[x])
-        copy.start()
-        stores.append(copy)
-    for copy in copies1 + copies2:
+    def edges2(along_x):
+        for i in range(1, 19):
+            c = VELOCITIES[i]
+            if c[2] == 0 or not c[0 if along_x else 1]:
+                continue
+            g = Z_PAIR[i]
+            for k in range(2):
+                if c[0]:
+                    x = X - 1 if c[0] > 0 else 0
+                    plane = 0 if c[0] > 0 else X + 1
+                    for t in range(YT):
+                        row = T * (1 + t)
+                        put2(came2(-c[0], 0, -c[2], x // half), k, g, x, t, plane, slice(row, row + T))
+                else:
+                    t = YT - 1 if c[1] > 0 else 0
+                    rows = low_halo if c[1] > 0 else high_halo
+                    for x in range(X):
+                        put2(came2(0, -c[1], -c[2], x // half), k, g, x, t, 1 + x, rows)
+
+    edges2(False)
+    for x in range(1, X - 1):
+        stream(x, False)
+    await2((1, 0, 1))
+    edges2(True)
+    for x in (0, X - 1):
+        stream(x, False)
+    for copy in list(copies1.values()) + raw + copies2:
         copy.wait_send()
-    for copy in stores:
-        copy.wait()
 
 
 def body(populations, solid):
@@ -344,13 +412,12 @@
     dma = pltpu.SemaphoreType.DMA
     return pl.pallas_call(
         step_kernel,
-        out_shape=jax.ShapeDtypeStruct(populations.shape, f32),
+        out_shape=pltpu.VMEM(populations.shape, f32),
         in_specs=[pl.BlockSpec(memory_space=pl.ANY)] * 2,
-        out_specs=pl.BlockSpec(memory_space=pl.ANY),
+        out_specs=pl.BlockSpec(memory_space=pltpu.VMEM),
         scratch_shapes=[
             pltpu.VMEM(populations.shape, f32),
             pltpu.VMEM(solid.shape, jnp.int32),
-            pltpu.VMEM(populations.shape, f32),
             pltpu.VMEM((2, X + 2, Y + 2 * T, Z), f32),
             pltpu.VMEM((2, X + 2, Y + 2 * T, Z), f32),
             pltpu.VMEM((2, 19, X + 2, Y + 2 * T, Z), f32),
@@ -361,10 +428,11 @@
             pltpu.VMEM((10, T, LANES), f32),
             pltpu.VMEM((2, T, LANES), f32),
             pltpu.VMEM((10, 2, T, LANES), f32),
+            pltpu.VMEM((2, 6, Y, Z), f32),
+            pltpu.VMEM((2, 6, Y, Z), f32),
             dma((X + 1,)),
-            dma((X,)),
-            dma((18,)),
-            dma((18,)),
+            dma((28,)),
+            dma((28,)),
             dma((26,)),
             dma((26,)),
         ],

time: 22.2 us -> 19.6 us (0.88)
  local copies, waits for them, and re-layouts: 2.47 us -> 1.04 us
  Pallas kernels: 19.6 us -> 18.4 us
    unnamed x1, local copies, waits for them, and re-layouts: 2.47 us -> 1.04 us
    pallas_call x1, Pallas kernels: 19.6 us -> 18.4 us  [body(): pl.pallas_call(step_kernel, out_shape=pltpu.VMEM(populations.shape, f32),...]
where the time goes in v2:
time: 19.6 us; the launch traced here: 19.5 us
  Pallas kernels  18.4 us (94%)
  local copies, waits for them, and re-layouts  1.04 us (5%)
    pallas_call x1, Pallas kernels, body(): pl.pallas_call(step_kernel, out_shape=pltpu.VMEM(populations.shape, f32),...  18.4 us
    unnamed x1, local copies, waits for them, and re-layouts  1.04 us

profile of v2, /device:TPU:0, one launch (start us, length us, event | category | flops | bytes accessed | tf_op | source)
XLA Modules:
  0.0 19.5 jit_solution(4857787747681378001)
XLA Ops:
  0.0 18.4 %shard_map.28 = f32[2,19,4,16,128]{4,3,2,1,0:T(8,128)S(1)} custom-call(f32[2,19,4,16,128]{4,3,2,1,0:T(8,128)} %pop_hbm.1, s32[4,16,128]{2,1,0:T(8,128)} %solid_hbm.1), custom_call_target="tpu_custom_call" | custom-call | tf_op jit(solution)/shard_map/pallas_call | solution.py:413
  18.4 1.0 %copy.4 = f32[2,19,4,16,128]{4,3,2,1,0:T(8,128)} copy(f32[2,19,4,16,128]{4,3,2,1,0:T(8,128)S(1)} %shard_map.28) | data formatting | bytes 2490368

commit v3 on v2

--- a/solution.py
+++ b/solution.py
@@ -65,19 +65,19 @@
         pltpu.make_async_copy(pop_hbm.at[:, :, x], pop.at[:, :, x], load_sem.at[x])
         for x in range(X)
     ]
+
+    me = [lax.axis_index(a) for a in AXES]
+    count = [lax.axis_size(a) for a in AXES]
+
+    def device(offset):
+        return tuple(lax.rem(me[d] + offset[d] + count[d], count[d]) for d in range(3))
+
+    barrier = pltpu.get_barrier_semaphore()
+    greeted = sorted(VELOCITIES[1:], key=lambda v: (-abs(v[2]), -abs(v[0]), -abs(v[1])))
+    for offset in greeted:
+        pl.semaphore_signal(barrier, inc=1, device_id=device(offset), device_id_type=MESH)
     for copy in loads:
         copy.start()
-
-    me = [lax.axis_index(a) for a in AXES]
-    count = [lax.axis_size(a) for a in AXES]
-
-    def device(offset):
-        return tuple(lax.rem(me[d] + offset[d] + count[d], count[d]) for d in range(3))
-
-    barrier = pltpu.get_barrier_semaphore()
-    greeted = [v for v in VELOCITIES[1:] if not (v[0] and v[2])]
-    for offset in greeted:
-        pl.semaphore_signal(barrier, inc=1, device_id=device(offset), device_id_type=MESH)
 
     lane = lax.broadcasted_iota(jnp.int32, (T, LANES), 1)
     pair = lane // 2
@@ -146,7 +146,7 @@
 
     order = sorted(range(1, 19), key=lambda i: -sum(abs(c) for c in VELOCITIES[i][::2]))
     copies1 = {}
-    for offset in sorted(greeted, key=lambda v: (-abs(v[2]), abs(v[0]) + abs(v[1]))):
+    for offset in sorted(greeted, key=lambda v: (-abs(v[2]), -abs(v[0]), -abs(v[1]))):
         n = len(copies1)
         if offset[2]:
             copy = remote(pack1, recv1.at[Z_INDEX[offset]], send1, got1, n, offset)
@@ -166,13 +166,8 @@
                 raw.append(copy)
     for dz in (1, -1):
         copies1[(0, 0, dz)].wait_recv()
-        for dx in (1, -1):
-            copy = remote(recv1.at[Z_INDEX[(0, 0, dz)]], recv1.at[Z_INDEX[(dx, 0, dz)]],
-                          send1, got1, len(copies1), (dx, 0, 0))
-            copy.start()
-            copies1[(dx, 0, dz)] = copy
     for offset in greeted:
-        if offset[:2] != (0, 0):
+        if offset[:2] != (0, 0) and not (offset[0] and offset[2]):
             copies1[offset].wait_recv()
 
     def came1(x, y, z):

time: 19.6 us -> 19.1 us (0.974)
  Pallas kernels: 18.4 us -> 17.9 us
    pallas_call x1, Pallas kernels: 18.4 us -> 17.9 us  [body(): pl.pallas_call(step_kernel, out_shape=pltpu.VMEM(populations.shape, f32),...]
where the time goes in v3:
time: 19.1 us; the launch traced here: 18.9 us
  Pallas kernels  17.9 us (94%)
  local copies, waits for them, and re-layouts  1.04 us (5%)
    pallas_call x1, Pallas kernels, body(): pl.pallas_call(step_kernel, out_shape=pltpu.VMEM(populations.shape, f32),...  17.9 us
    unnamed x1, local copies, waits for them, and re-layouts  1.04 us

profile of v3, /device:TPU:0, one launch (start us, length us, event | category | flops | bytes accessed | tf_op | source)
XLA Modules:
  0.0 18.9 jit_solution(15606417137851025467)
XLA Ops:
  0.0 17.9 %shard_map.28 = f32[2,19,4,16,128]{4,3,2,1,0:T(8,128)S(1)} custom-call(f32[2,19,4,16,128]{4,3,2,1,0:T(8,128)} %pop_hbm.1, s32[4,16,128]{2,1,0:T(8,128)} %solid_hbm.1), custom_call_target="tpu_custom_call" | custom-call | tf_op jit(solution)/shard_map/pallas_call | solution.py:408
  17.9 1.0 %copy.4 = f32[2,19,4,16,128]{4,3,2,1,0:T(8,128)} copy(f32[2,19,4,16,128]{4,3,2,1,0:T(8,128)S(1)} %shard_map.28) | data formatting | bytes 2490368
